TPU v7x, 32 devices: a whole 2x2x4 slice. The times are simulated.
32 devices in a mesh: dp: 2 (over core), row: 4 (over y, x), col: 4 (over z).
Axes of the slice: x: 2, y: 2, z: 4, core: 2. Of those that a mesh axis runs over, the one named last changes fastest.
Arguments:
- block_input: float32 [4096, 2048], P(('dp', 'row'), 'col'), as said below
- out_grad: float32 [4096, 2048], P(('dp', 'row'), 'col'), may hold values from -6 to 6
- ln1_gain: float32 [2048], P('col'), may hold values from 0.25 to 1.75
- ln1_bias: float32 [2048], P('col'), may hold values from -1.75 to 1.75
- ln2_gain: float32 [2048], P('col'), may hold values from 0.25 to 1.75
- ln2_bias: float32 [2048], P('col'), may hold values from -1.75 to 1.75
- w_qkv: bfloat16 [2048, 6144], P('row', 'col'), as said below
- b_qkv: float32 [6144], P('col'), may hold values from -3 to 3
- w_dense: bfloat16 [2048, 2048], P('col', 'row'), may hold values from -0.5 to 0.5
- b_dense: float32 [2048], P('col'), may hold values from -1.75 to 1.75
- w_fc: bfloat16 [2048, 8192], P('row', 'col'), may hold values from -0.125 to 0.125
- b_fc: float32 [8192], P('col'), may hold values from -3 to 3
- w_proj: bfloat16 [8192, 2048], P('col', 'row'), may hold values from -0.0625 to 0.0625
- b_proj: float32 [2048], P('col'), may hold values from -1.75 to 1.75
Outputs:
- block_output: float32 [4096, 2048], P(('dp', 'row'), 'col')
- input_grad: float32 [4096, 2048], P(('dp', 'row'), 'col')
- grad_ln1_gain: float32 [2048], P('col')
- grad_ln1_bias: float32 [2048], P('col')
- grad_ln2_gain: float32 [2048], P('col')
- grad_ln2_bias: float32 [2048], P('col')
- grad_w_qkv: float32 [2048, 6144], P('row', 'col')
- grad_b_qkv: float32 [6144], P('col')
- grad_w_dense: float32 [2048, 2048], P('col', 'row')
- grad_b_dense: float32 [2048], P('col')
- grad_w_fc: float32 [2048, 8192], P('row', 'col')
- grad_b_fc: float32 [8192], P('col')
- grad_w_proj: float32 [8192, 2048], P('col', 'row')
- grad_b_proj: float32 [2048], P('col')
Inputs may be any that keep to these rules, and one draw needn't show every extreme that they name: `block_input`: finite real values. `w_qkv`: finite real values.
All inputs are finite; a program needn't handle non-finite values.
Results may differ from a plain program's by a relative error of at most 0.011.
Values may be sent and summed in bfloat16 or wider, within the bound.
A program may use at most 320 MiB of HBM per device.

v0:
```python
import math
import jax
import jax.numpy as jnp
from jax import lax
from jax.sharding import PartitionSpec as P

D = 2048
HD = 256
ROT = 64
SEQ = 512
epsilon = 1e-05
contract_last = (((1,), (1,)), ((), ()))
contract_first = (((0,), (0,)), ((), ()))


def angle_tables(length):
    half_rot = ROT // 2
    position = jnp.arange(length, dtype=jnp.float32)
    exponent = jnp.arange(half_rot, dtype=jnp.float32) * (2.0 / ROT)
    frequency = 10000.0 ** (-exponent)
    angles = position[:, None] * frequency[None, :]
    return (jnp.cos(angles), jnp.sin(angles))


def rotate_fwd(values, cosine, sine_vals):
    half_rot = ROT // 2
    first = values[..., :half_rot]
    second = values[..., half_rot:ROT]
    cos_part = cosine[:, None, :]
    sin_part = sine_vals[:, None, :]
    return jnp.concatenate(
        [
            first * cos_part - second * sin_part,
            second * cos_part + first * sin_part,
            values[..., ROT:],
        ],
        axis=-1,
    )


def rotate_back(grads, cosine, sine_vals):
    half_rot = ROT // 2
    first = grads[..., :half_rot]
    second = grads[..., half_rot:ROT]
    cos_part = cosine[:, None, :]
    sin_part = sine_vals[:, None, :]
    return jnp.concatenate(
        [
            first * cos_part + second * sin_part,
            second * cos_part - first * sin_part,
            grads[..., ROT:],
        ],
        axis=-1,
    )


def gelu_value(pre_act):
    return 0.5 * pre_act * (1.0 + lax.erf(pre_act * 0.7071067811865476))


def gelu_slope(pre_act):
    return 0.5 * (
        1.0 + lax.erf(pre_act * 0.7071067811865476)
    ) + pre_act * 0.3989422804014327 * jnp.exp(-0.5 * pre_act * pre_act)


def shards(
    block_input,
    out_grad,
    ln1_gain,
    ln1_bias,
    ln2_gain,
    ln2_bias,
    w_qkv,
    b_qkv,
    w_dense,
    b_dense,
    w_fc,
    b_fc,
    w_proj,
    b_proj,
):
    tok_rows = block_input.shape[0]
    seq_count = tok_rows // SEQ
    qkv_cols = w_qkv.shape[1]
    fc_cols = w_fc.shape[1]
    local_heads = qkv_cols // (3 * HD)
    head_cols = local_heads * HD
    scale = 1.0 / math.sqrt(HD)
    cosine, sine_vals = angle_tables(SEQ)
    causal = jnp.arange(SEQ)[:, None] >= jnp.arange(SEQ)[None, :]
    row_total, square_total = lax.psum(
        (jnp.sum(block_input, axis=1), jnp.sum(block_input * block_input, axis=1)), "col"
    )
    mean_row = (row_total / D)[:, None]
    var_row = (square_total / D)[:, None] - mean_row * mean_row
    inv_std = lax.rsqrt(var_row + epsilon)
    x_hat = (block_input - mean_row) * inv_std
    normed_one = (x_hat * ln1_gain + ln1_bias).astype(jnp.bfloat16)
    normed_two = (x_hat * ln2_gain + ln2_bias).astype(jnp.bfloat16)
    wide_one, wide_two = (
        lax.all_gather(normed_one, "col", axis=1, tiled=True),
        lax.all_gather(normed_two, "col", axis=1, tiled=True),
    )
    part_one = wide_one
    part_two = wide_two
    qkv_pre = jnp.dot(
        part_one,
        lax.all_gather(w_qkv, "row", axis=0, tiled=True),
        preferred_element_type=jnp.float32,
    )
    fc_pre = jnp.dot(
        part_two,
        lax.all_gather(w_fc, "row", axis=0, tiled=True),
        preferred_element_type=jnp.float32,
    )
    qkv_pre = qkv_pre + b_qkv
    fc_pre = fc_pre + b_fc

    def forward_seq(block):
        query = rotate_fwd(block[:, :, 0], cosine, sine_vals).astype(jnp.bfloat16)
        keys = rotate_fwd(block[:, :, 1], cosine, sine_vals).astype(jnp.bfloat16)
        values = block[:, :, 2].astype(jnp.bfloat16)
        scores = jnp.einsum("qhd,khd->hqk", query, keys, preferred_element_type=jnp.float32) * scale
        masked = jnp.where(causal[None], scores, -1e30)
        row_max = jnp.max(masked, axis=-1, keepdims=True)
        exp_sum = jnp.sum(
            jnp.where(causal[None], jnp.exp(masked - row_max), 0.0), axis=-1, keepdims=True
        )
        log_total = row_max + jnp.log(exp_sum)
        probs_low = jnp.where(causal[None], jnp.exp(masked - log_total), 0.0).astype(jnp.bfloat16)
        attended = jnp.einsum(
            "hqk,khd->qhd", probs_low, values, preferred_element_type=jnp.float32
        ).astype(jnp.bfloat16)
        return (query, keys, values, attended, log_total)

    query, keys, values, attended, log_total = lax.map(
        forward_seq, qkv_pre.reshape(seq_count, SEQ, local_heads, 3, HD)
    )
    attn_out = attended.reshape(tok_rows, head_cols)
    gelu_out = gelu_value(fc_pre).astype(jnp.bfloat16)
    out_stack = jnp.concatenate([w_dense, w_proj], axis=0)
    shard_piece = lax.all_gather(out_stack, "row", axis=1, tiled=True)
    mixed = jnp.dot(
        attn_out, shard_piece[:head_cols], preferred_element_type=jnp.float32
    ) + jnp.dot(gelu_out, shard_piece[head_cols:], preferred_element_type=jnp.float32)
    branch_sum = lax.psum_scatter(mixed, "col", scatter_dimension=1, tiled=True)
    block_output = block_input + branch_sum + b_dense + b_proj
    grad_low = out_grad.astype(jnp.bfloat16)
    wide_grad = lax.all_gather(grad_low, "col", axis=1, tiled=True)
    both_grad = lax.dot_general(
        wide_grad,
        lax.all_gather(out_stack, "row", axis=1, tiled=True),
        contract_last,
        preferred_element_type=jnp.float32,
    )
    attn_grad = both_grad[:, :head_cols]
    gelu_grad = both_grad[:, head_cols:]
    attn_grad_low = attn_grad.astype(jnp.bfloat16)
    fc_grad = gelu_grad * gelu_slope(fc_pre)
    fc_bias_grad = jnp.sum(fc_grad, axis=0)
    fc_grad_low = fc_grad.astype(jnp.bfloat16)

    def backward_seq(items):
        query_s, keys_s, values_s, attended_s, log_s, head_grad = items
        scores = (
            jnp.einsum("qhd,khd->hqk", query_s, keys_s, preferred_element_type=jnp.float32) * scale
        )
        probs = jnp.where(
            causal[None], jnp.exp(jnp.where(causal[None], scores, -1e30) - log_s), 0.0
        )
        probs_low = probs.astype(jnp.bfloat16)
        value_grad = jnp.einsum(
            "hqk,qhd->khd", probs_low, head_grad, preferred_element_type=jnp.float32
        )
        prob_grad = jnp.einsum(
            "qhd,khd->hqk", head_grad, values_s, preferred_element_type=jnp.float32
        )
        delta_row = jnp.transpose(
            jnp.sum(head_grad.astype(jnp.float32) * attended_s.astype(jnp.float32), axis=-1), (1, 0)
        )[:, :, None]
        score_grad = (probs * (prob_grad - delta_row) * scale).astype(jnp.bfloat16)
        query_grad = jnp.einsum(
            "hqk,khd->qhd", score_grad, keys_s, preferred_element_type=jnp.float32
        )
        key_grad = jnp.einsum(
            "hqk,qhd->khd", score_grad, query_s, preferred_element_type=jnp.float32
        )
        return jnp.stack(
            [
                rotate_back(query_grad, cosine, sine_vals),
                rotate_back(key_grad, cosine, sine_vals),
                value_grad,
            ],
            axis=2,
        )

    head_grads = attn_grad_low.reshape(seq_count, SEQ, local_heads, HD)
    qkv_grad = lax.map(
        backward_seq, (query, keys, values, attended, log_total, head_grads)
    ).reshape(tok_rows, qkv_cols)
    qkv_bias_grad = jnp.sum(qkv_grad, axis=0)
    qkv_grad_low = qkv_grad.astype(jnp.bfloat16)
    in_stack = jnp.concatenate([w_qkv, w_fc], axis=1)
    shard_piece = lax.all_gather(in_stack, "row", axis=0, tiled=True)
    norm_grads = jnp.stack(
        [
            lax.dot_general(
                qkv_grad_low,
                shard_piece[:, :qkv_cols],
                contract_last,
                preferred_element_type=jnp.float32,
            ),
            lax.dot_general(
                fc_grad_low,
                shard_piece[:, qkv_cols:],
                contract_last,
                preferred_element_type=jnp.float32,
            ),
        ]
    )
    part_one = wide_one
    part_two = wide_two
    row_part = lax.psum_scatter(
        jnp.concatenate(
            [
                lax.dot_general(
                    part_one, qkv_grad_low, contract_first, preferred_element_type=jnp.float32
                ),
                lax.dot_general(
                    part_two, fc_grad_low, contract_first, preferred_element_type=jnp.float32
                ),
                lax.dot_general(
                    wide_grad, attn_out, contract_first, preferred_element_type=jnp.float32
                ),
                lax.dot_general(
                    wide_grad, gelu_out, contract_first, preferred_element_type=jnp.float32
                ),
            ],
            axis=1,
        ),
        "row",
        scatter_dimension=0,
        tiled=True,
    )
    grad_rows = lax.psum(row_part, "dp")
    qkv_total = grad_rows[:, :qkv_cols]
    fc_total = grad_rows[:, qkv_cols : qkv_cols + fc_cols]
    dense_total = grad_rows[:, qkv_cols + fc_cols : qkv_cols + fc_cols + head_cols].T
    proj_total = grad_rows[:, qkv_cols + fc_cols + head_cols :].T
    norm_local = lax.psum_scatter(norm_grads, "col", scatter_dimension=2, tiled=True)
    grad_one = norm_local[0]
    grad_two = norm_local[1]
    hat_grad = grad_one * ln1_gain + grad_two * ln2_gain
    total_hat, total_cross = lax.psum(
        (jnp.sum(hat_grad, axis=1), jnp.sum(hat_grad * x_hat, axis=1)), "col"
    )
    input_grad = out_grad + inv_std * (
        hat_grad - (total_hat / D)[:, None] - x_hat * (total_cross / D)[:, None]
    )
    gain_one, shift_one, gain_two, shift_two, qkv_bias_total, fc_bias_total, out_bias_total = (
        lax.psum(
            (
                jnp.sum(grad_one * x_hat, axis=0),
                jnp.sum(grad_one, axis=0),
                jnp.sum(grad_two * x_hat, axis=0),
                jnp.sum(grad_two, axis=0),
                qkv_bias_grad,
                fc_bias_grad,
                jnp.sum(out_grad, axis=0),
            ),
            ("dp", "row"),
        )
    )
    return (
        block_output,
        input_grad,
        gain_one,
        shift_one,
        gain_two,
        shift_two,
        qkv_total,
        qkv_bias_total,
        dense_total,
        out_bias_total,
        fc_total,
        fc_bias_total,
        proj_total,
        out_bias_total,
    )


def solution(mesh):
    return jax.shard_map(
        shards,
        mesh=mesh,
        in_specs=(
            P(("dp", "row"), "col"),
            P(("dp", "row"), "col"),
            P("col"),
            P("col"),
            P("col"),
            P("col"),
            P("row", "col"),
            P("col"),
            P("col", "row"),
            P("col"),
            P("row", "col"),
            P("col"),
            P("col", "row"),
            P("col"),
        ),
        out_specs=(
            P(("dp", "row"), "col"),
            P(("dp", "row"), "col"),
            P("col"),
            P("col"),
            P("col"),
            P("col"),
            P("row", "col"),
            P("col"),
            P("col", "row"),
            P("col"),
            P("row", "col"),
            P("col"),
            P("col", "row"),
            P("col"),
        ),
        check_vma=False,
    )
```

profile of v0, /device:TPU:0, one launch (start us, length us, event | category | flops | bytes accessed | tf_op | source)
XLA Modules:
  0.0 1304.8 jit_solution(7486907103567437499)
XLA Ops:
  8.9 13.5 %all-reduce.2 = (f32[512]{0:T(512)S(1)}, f32[512]{0:T(512)S(1)}) all-reduce(f32[512]{0:T(512)S(1)} %get-tuple-element.126, f32[512]{0:T(512)S(1)} %get-tuple-element.125), channel_id=1, replica_groups=mesh['dp'=2,'row'=4,'col'=4] {'col'}, use_global_device_ids=true, to_apply=%region_3.0 | all-reduce | flops 1024 | bytes 8192 | tf_op jit(solution)/shard_map/psum | solution.py:92
  27.3 3.4 pad_maximum_fusion.4
  32.0 3.6 pad_maximum_fusion.2
  38.1 30.9 %all-gather.8.cloned.1.call-done = bf16[512,2048]{1,0:T(8,128)(2,1)} async-done(((bf16[512,512]{1,0:T(8,128)(2,1)}), bf16[512,2048]{1,0:T(8,128)(2,1)}) %all-gather.8.cloned.1.call-update) | async-done | bytes 2097168 | tf_op jit(solution)/shard_map/all_gather | solution.py:102
  69.0 70.7 %all-gather.10.cloned.1.call-done = bf16[2048,1536]{1,0:T(8,128)(2,1)} async-done(((bf16[512,1536]{1,0:T(8,128)(2,1)}), bf16[2048,1536]{1,0:T(8,128)(2,1)}) %all-gather.10.cloned.1.call-update) | async-done | bytes 6291472 | tf_op jit(solution)/shard_map/all_gather | solution.py:109
  139.7 8.5 convolution_add_fusion.1
  166.4 21.1 %all-gather.18.cloned.1.call-done = bf16[512,2048]{1,0:T(8,128)(2,1)} async-done(((bf16[512,512]{1,0:T(8,128)(2,1)}), bf16[512,2048]{1,0:T(8,128)(2,1)}) %all-gather.18.cloned.1.call-update) | async-done | bytes 2097168 | tf_op jit(solution)/shard_map/all_gather | solution.py:150
  187.5 105.9 %all-gather.12.cloned.1.call-done = bf16[2560,2048]{1,0:T(8,128)(2,1)} async-done(((bf16[2560,512]{1,0:T(8,128)(2,1)}), bf16[2560,2048]{1,0:T(8,128)(2,1)}) %all-gather.12.cloned.1.call-update) | async-done | bytes 10485776 | tf_op jit(solution)/shard_map/all_gather | solution.py:143
  293.4 9.5 convolution_bitcast_fusion.1
  308.3 3.4 multiply_reduce_fusion.1
  321.8 5.0 convolution_bitcast_fusion.2
  326.8 6.3 fusion.42
  333.1 7.4 all-gather.14.cloned.1.call-done
  340.5 88.0 %all-gather.16.cloned.1.call-done = bf16[2048,2048]{1,0:T(8,128)(2,1)} async-done(((bf16[512,2048]{1,0:T(8,128)(2,1)}), bf16[2048,2048]{1,0:T(8,128)(2,1)}) %all-gather.16.cloned.1.call-update) | async-done | bytes 8388624 | tf_op jit(solution)/shard_map/all_gather | solution.py:114
  428.6 9.9 fusion.36
  438.5 9.2 fusion.23
  448.2 8.3 convolution_bitcast_fusion
  456.5 32.9 %pad_maximum_fusion = f32[2048,6144]{0,1:T(8,128)} fusion(f32[2048,2048]{0,1:T(8,128)} %convolution_bitcast_fusion, f32[2048,512]{0,1:T(8,128)S(1)} %copy-done, f32[2048,2048]{0,1:T(8,128)} %fusion.23, f32[2048,1536]{0,1:T(8,128)} %fusion.42), kind=kLoop, calls=%fused_computation | loop fusion | flops 37748736 | bytes 100663296 | tf_op jit(solution)/shard_map/concatenate | solution.py:225
  489.4 80.8 %all-gather.20.cloned.1.call-done = bf16[2048,3584]{1,0:T(8,128)(2,1)} async-done(((bf16[512,3584]{1,0:T(8,128)(2,1)}), bf16[2048,3584]{1,0:T(8,128)(2,1)}) %all-gather.20.cloned.1.call-update) | async-done | bytes 14680080 | tf_op jit(solution)/shard_map/all_gather | solution.py:205
  570.3 6.2 fusion.10
  576.5 7.0 fusion.13
  583.5 3.8 pad_maximum_fusion.1
  587.6 9.5 fusion.2
  597.0 5.0 convolution_add_fusion
  602.1 395.2 %reduce-scatter.8.cloned.1.call-done = f32[512,6144]{0,1:T(8,128)} async-done(((f32[2048,6144]{0,1:T(8,128)}), f32[512,6144]{0,1:T(8,128)}) %reduce-scatter.8.cloned.1.call-update) | async-done | bytes 12582928 | tf_op jit(solution)/shard_map/reduce_scatter | solution.py:224
  999.0 145.4 %reduce-scatter.6.cloned.1.call-done = f32[2,512,512]{2,1,0:T(8,128)} async-done(((f32[2,512,2048]{2,1,0:T(8,128)}), f32[2,512,512]{2,1,0:T(8,128)}) %reduce-scatter.6.cloned.1.call-update) | async-done | bytes 2097168 | tf_op jit(solution)/shard_map/reduce_scatter | solution.py:251
  1148.3 27.5 %all-reduce = (f32[512]{0:T(512)}, f32[512]{0:T(512)}, f32[512]{0:T(512)}, f32[512]{0:T(512)}, f32[1536]{0:T(1024)}, /*index=5*/f32[512]{0:T(512)S(1)}, f32[2048]{0:T(1024)}) all-reduce(f32[512]{0:T(512)S(1)} %get-tuple-element.120, f32[512]{0:T(512)S(1)} %get-tuple-element.122, ...), channel_id=1, replica_groups=mesh['dp'=2,'row'=4,'col'=4] {'dp','row'}, use_global_device_ids=true, to_apply=%region_14.15 | all-reduce | flops 6144 | bytes 49152 | tf_op jit(solution)/shard_map/psum | solution.py:262
  1175.8 12.4 all-reduce.1
  1188.2 36.5 %reduce-scatter.4.cloned.1.call-done = f32[512,512]{1,0:T(8,128)} async-done(((f32[512,2048]{1,0:T(8,128)}), f32[512,512]{1,0:T(8,128)}) %reduce-scatter.4.cloned.1.call-update) | async-done | bytes 1048592 | tf_op jit(solution)/shard_map/reduce_scatter | solution.py:147
  1227.7 50.2 %all-reduce.5.cloned.1.call-done = f32[512,6144]{0,1:T(8,128)} async-done(((f32[512,6144]{0,1:T(8,128)}), f32[512,6144]{0,1:T(8,128)}) %all-reduce.5.cloned.1.call-update) | async-done | bytes 12582928 | tf_op jit(solution)/shard_map/psum | solution.py:246
  1282.1 7.7 slice_bitcast_fusion
  1289.8 5.3 copy.89
  (156 shorter events, 60.0 us)
Async XLA Ops:
  7.2 18.6 %copy-start.6 = (f32[512,512]{1,0:T(8,128)S(1)}, f32[512,512]{1,0:T(8,128)}, u32[]{:S(2)}) copy-start(f32[512,512]{1,0:T(8,128)} %param.15) | copy-start | bytes 3145732
  7.2 20.1 %copy-start.27 = (bf16[512,512]{1,0:T(8,128)(2,1)S(1)}, bf16[512,512]{1,0:T(8,128)(2,1)}, u32[]{:S(2)}) copy-start(bf16[512,512]{1,0:T(8,128)(2,1)} %param.22) | copy-start | bytes 1572868
  7.2 61.8 %all-gather.8.cloned.1.call-start = ((), (), s32[]{:S(2)}) async-start(), calls=%async_computation.3 | async-start | bytes 2621440 | tf_op jit(solution)/shard_map/all_gather | solution.py:102
  25.0 114.7 %all-gather.10.cloned.1.call-start = ((), (), s32[]{:S(2)}) async-start(), calls=%async_computation.4 | async-start | bytes 7864320 | tf_op jit(solution)/shard_map/all_gather | solution.py:109
  25.7 161.8 %all-gather.18.cloned.1.call-start = ((), (), s32[]{:S(2)}) async-start(), calls=%async_computation.9 | async-start | bytes 2621440 | tf_op jit(solution)/shard_map/all_gather | solution.py:150
  27.3 266.2 %all-gather.12.cloned.1.call-start = ((), (), s32[]{:S(2)}) async-start(), calls=%async_computation.5 | async-start | bytes 13107200 | tf_op jit(solution)/shard_map/all_gather | solution.py:143
  30.7 309.8 %all-gather.14.cloned.1.call-start = ((), (), s32[]{:S(2)}) async-start(), calls=%async_computation.6 | async-start | bytes 2621440 | tf_op jit(solution)/shard_map/all_gather | solution.py:103
  31.3 397.2 %all-gather.16.cloned.1.call-start = ((), (), s32[]{:S(2)}) async-start(), calls=%async_computation.7 | async-start | bytes 10485760 | tf_op jit(solution)/shard_map/all_gather | solution.py:114
  31.9 107.8 %copy-start.41 = (f32[1536]{0:T(1024)S(1)}, f32[1536]{0:T(1024)}, u32[]{:S(2)}) copy-start(f32[1536]{0:T(1024)} %param.21) | copy-start | bytes 18436
  31.9 538.3 %all-gather.20.cloned.1.call-start = ((), (), s32[]{:S(2)}) async-start(), calls=%async_computation.10 | async-start | bytes 18350080 | tf_op jit(solution)/shard_map/all_gather | solution.py:205
  35.6 961.8 %reduce-scatter.8.cloned.1.call-start = ((), (), s32[]{:S(2)}) async-start(), calls=%async_computation.12 | async-start | bytes 62914560 | tf_op jit(solution)/shard_map/reduce_scatter | solution.py:224
  321.7 5.0 copy-start.39
  326.8 101.8 %copy-start.42 = (f32[2048]{0:T(1024)S(1)}, f32[2048]{0:T(1024)}, u32[]{:S(2)}) copy-start(f32[2048]{0:T(1024)} %param.25) | copy-start | bytes 24580
  428.6 9.9 copy-start.40
  438.5 9.2 copy-start.43
  438.5 9.7 copy-start.45
  438.5 9.7 copy-start.13
  448.2 8.3 copy-start
  489.4 655.0 %reduce-scatter.6.cloned.1.call-start = ((), (), s32[]{:S(2)}) async-start(), calls=%async_computation.11 | async-start | bytes 10485760 | tf_op jit(solution)/shard_map/reduce_scatter | solution.py:251
  570.3 6.2 copy-start.44
  587.3 637.4 %reduce-scatter.4.cloned.1.call-start = ((), (), s32[]{:S(2)}) async-start(), calls=%async_computation.8 | async-start | bytes 5242880 | tf_op jit(solution)/shard_map/reduce_scatter | solution.py:147
  602.0 675.8 %all-reduce.5.cloned.1.call-start = ((), (), s32[]{:S(2)}) async-start(), calls=%async_computation.13 | async-start | bytes 25165824 | tf_op jit(solution)/shard_map/psum | solution.py:246
  997.4 148.7 %copy-start.1 = (f32[512,512]{1,0:T(8,128)S(1)}, f32[512,512]{1,0:T(8,128)}, u32[]{:S(2)}) copy-start(f32[512,512]{1,0:T(8,128)} %param.14) | copy-start | bytes 3145732
  997.4 148.7 %copy-start.30 = (f32[512]{0:T(512)S(1)}, f32[512]{0:T(512)}, u32[]{:S(2)}) copy-start(f32[512]{0:T(512)} %copy-done.29) | copy-start | bytes 6148
  997.4 148.7 %copy-start.32 = (f32[512]{0:T(512)S(1)}, f32[512]{0:T(512)}, u32[]{:S(2)}) copy-start(f32[512]{0:T(512)} %copy-done.31) | copy-start | bytes 6148
  997.4 148.7 %copy-start.34 = (f32[512]{0:T(512)S(1)}, f32[512]{0:T(512)}, u32[]{:S(2)}) copy-start(f32[512]{0:T(512)} %param.16) | copy-start | bytes 6148
  997.4 148.7 %copy-start.35 = (f32[512]{0:T(512)S(1)}, f32[512]{0:T(512)}, u32[]{:S(2)}) copy-start(f32[512]{0:T(512)} %param.18) | copy-start | bytes 6148
  997.4 150.9 %copy-start.33 = (f32[512]{0:T(512)S(1)}, f32[512]{0:T(512)}, u32[]{:S(2)}) copy-start(f32[512]{0:T(512)} %get-tuple-element.155) | copy-start | bytes 6148
  997.4 227.3 %copy-start.36 = (f32[512]{0:T(512)S(1)}, f32[512]{0:T(512)}, u32[]{:S(2)}) copy-start(f32[512]{0:T(512)} %param.27) | copy-start | bytes 6148
  997.4 227.3 %copy-start.37 = (f32[512]{0:T(512)S(1)}, f32[512]{0:T(512)}, u32[]{:S(2)}) copy-start(f32[512]{0:T(512)} %param.23) | copy-start | bytes 6148
  998.9 225.8 %copy-start.7 = (f32[512,512]{1,0:T(8,128)S(1)}, f32[512,512]{1,0:T(8,128)}, u32[]{:S(2)}) copy-start(f32[512,512]{1,0:T(8,128)} %param.15) | copy-start | bytes 3145732
  1175.8 121.7 %copy-start.38 = (f32[512]{0:T(512)}, f32[512]{0:T(512)S(1)}, u32[]{:S(2)}) copy-start(f32[512]{0:T(512)S(1)} %get-tuple-element.204) | copy-start | bytes 6148
  (26 other events, 85.6 us)
Sparse Core Ops, SparseCore 0:
  25.1 43.8 all-gather.7
  70.8 68.8 all-gather.9
  141.8 45.6 all-gather.17
  189.8 103.5 all-gather.11
  294.8 45.6 all-gather.13
  342.2 86.2 all-gather.15
  430.4 139.8 all-gather.19
  573.4 423.9 reduce-scatter.7
  999.7 144.6 reduce-scatter.5
  1147.1 77.6 reduce-scatter.3
  1227.3 50.5 all-reduce.4
where the time goes:
time: 1310 us; the launch traced here: 1300 us
  waiting for transfers between devices  1030 us (79%)
  matrix products  91.9 us (7%)
  other arithmetic  65.9 us (5%)
  blocking collectives  53.4 us (4%)
  local copies, waits for them, and re-layouts  44.1 us (3%)
  between operations  14.7 us (1%)
    reduce_scatter x1, waiting for transfers between devices, shards(): lax.psum_scatter(jnp.concatenate([lax.dot_general(part_one, qkv_grad_low,...  395 us
    reduce_scatter x1, waiting for transfers between devices, shards(): lax.psum_scatter(norm_grads, 'col', scatter_dimension=2, tiled=True)  145 us
    all_gather x1, waiting for transfers between devices, shards(): shard_piece = lax.all_gather(out_stack, 'row', axis=1, tiled=True)  106 us
    all_gather x1, waiting for transfers between devices, shards(): lax.all_gather(w_fc, 'row', axis=0, tiled=True)  88 us
    all_gather x1, waiting for transfers between devices, shards(): shard_piece = lax.all_gather(in_stack, 'row', axis=0, tiled=True)  80.8 us
    all_gather x1, waiting for transfers between devices, shards(): lax.all_gather(w_qkv, 'row', axis=0, tiled=True)  70.7 us
    psum x1, waiting for transfers between devices, shards(): grad_rows = lax.psum(row_part, 'dp')  50.2 us
    reduce_scatter x1, waiting for transfers between devices, shards(): branch_sum = lax.psum_scatter(mixed, 'col', scatter_dimension=1, tiled=True)  36.5 us
  transfers between devices with their start and end apart: 11, of which 11 were waited for; matrix products, arithmetic and copies ran while one was open for 13% of the time, Pallas kernels for 0%

commit v1 on v0

--- a/solution.py
+++ b/solution.py
@@ -11,6 +11,18 @@
 epsilon = 1e-05
 contract_last = (((1,), (1,)), ((), ()))
 contract_first = (((0,), (0,)), ((), ()))
+
+
+def collect(x, axis, dim):
+    ways, here = (lax.axis_size(axis), lax.axis_index(axis))
+    grown, reach = (x, 1)
+    while reach < ways:
+        theirs = lax.ppermute(grown, axis, [(d, d ^ reach) for d in range(ways)])
+        mine_first = jnp.concatenate([grown, theirs], axis=dim)
+        theirs_first = jnp.concatenate([theirs, grown], axis=dim)
+        grown = jnp.where(here & reach == 0, mine_first, theirs_first)
+        reach = 2 * reach
+    return grown
 
 
 def angle_tables(length):
@@ -109,11 +121,7 @@
         lax.all_gather(w_qkv, "row", axis=0, tiled=True),
         preferred_element_type=jnp.float32,
     )
-    fc_pre = jnp.dot(
-        part_two,
-        lax.all_gather(w_fc, "row", axis=0, tiled=True),
-        preferred_element_type=jnp.float32,
-    )
+    fc_pre = jnp.dot(part_two, collect(w_fc, "row", 0), preferred_element_type=jnp.float32)
     qkv_pre = qkv_pre + b_qkv
     fc_pre = fc_pre + b_fc
 

time: 1310 us -> 1270 us (0.969)
  waiting for transfers between devices: 1030 us -> 982 us
    all_gather x1 -> x0, waiting for transfers between devices: 88 us -> none  [shards(): lax.all_gather(w_fc, 'row', axis=0, tiled=True)]
    ppermute x0 -> x2, waiting for transfers between devices: none -> 42.1 us  [collect(): theirs = lax.ppermute(grown, axis, [(d, d ^ reach) for d in range(ways)])]
    all_gather x1, waiting for transfers between devices: 30.9 us -> 0.01 us  [shards(): lax.all_gather(normed_one, 'col', axis=1, tiled=True)]
    all_gather x1, waiting for transfers between devices: 70.7 us -> 101 us  [shards(): lax.all_gather(w_qkv, 'row', axis=0, tiled=True)]
  transfers between devices with their start and end apart: 11 -> 12, of which waited for: 11 -> 10; matrix products, arithmetic and copies ran while one was open for 13% -> 14% of each run, Pallas kernels for 0% -> 0%
where the time goes in v1:
time: 1270 us; the launch traced here: 1260 us
  waiting for transfers between devices  982 us (77%)
  matrix products  94.5 us (7%)
  other arithmetic  72.6 us (6%)
  blocking collectives  53.3 us (4%)
  local copies, waits for them, and re-layouts  43.5 us (3%)
  between operations  15 us (1%)
    reduce_scatter x1, waiting for transfers between devices, shards(): lax.psum_scatter(jnp.concatenate([lax.dot_general(part_one, qkv_grad_low,...  395 us
    reduce_scatter x1, waiting for transfers between devices, shards(): lax.psum_scatter(norm_grads, 'col', scatter_dimension=2, tiled=True)  145 us
    all_gather x1, waiting for transfers between devices, shards(): shard_piece = lax.all_gather(out_stack, 'row', axis=1, tiled=True)  106 us
    all_gather x1, waiting for transfers between devices, shards(): lax.all_gather(w_qkv, 'row', axis=0, tiled=True)  101 us
    all_gather x1, waiting for transfers between devices, shards(): shard_piece = lax.all_gather(in_stack, 'row', axis=0, tiled=True)  76.3 us
    psum x1, waiting for transfers between devices, shards(): grad_rows = lax.psum(row_part, 'dp')  50 us
    ppermute x2, waiting for transfers between devices, collect(): theirs = lax.ppermute(grown, axis, [(d, d ^ reach) for d in range(ways)])  42.1 us
    reduce_scatter x1, waiting for transfers between devices, shards(): branch_sum = lax.psum_scatter(mixed, 'col', scatter_dimension=1, tiled=True)  36.8 us
  transfers between devices with their start and end apart: 12, of which 10 were waited for; matrix products, arithmetic and copies ran while one was open for 14% of the time, Pallas kernels for 0%

profile of v1, /device:TPU:0, one launch (start us, length us, event | category | flops | bytes accessed | tf_op | source)
XLA Modules:
  0.0 1263.7 jit_solution(15780885147799556896)
XLA Ops:
  8.9 13.5 %all-reduce.2 = (f32[512]{0:T(512)S(1)}, f32[512]{0:T(512)S(1)}) all-reduce(f32[512]{0:T(512)S(1)} %get-tuple-element.126, f32[512]{0:T(512)S(1)} %get-tuple-element.125), channel_id=1, replica_groups=mesh['dp'=2,'row'=4,'col'=4] {'col'}, use_global_device_ids=true, to_apply=%region_3.0 | all-reduce | flops 1024 | bytes 8192 | tf_op jit(solution)/shard_map/psum | solution.py:104
  27.3 3.4 pad_maximum_fusion.4
  31.4 3.7 pad_maximum_fusion.2
  39.2 42.1 %collective-permute-done = bf16[512,2048]{1,0:T(8,128)(2,1)} collective-permute-done((bf16[512,2048]{1,0:T(8,128)(2,1)S(1)}, bf16[512,2048]{1,0:T(8,128)(2,1)}, u32[]{:S(2)}, u32[]{:S(2)}) %collective-permute-start) | collective-permute-done | bytes 2097184 | tf_op jit(solution)/shard_map/ppermute | solution.py:20
  81.2 5.2 maximum_select_fusion.2
  87.5 100.8 %all-gather.9.cloned.1.call-done = bf16[2048,1536]{1,0:T(8,128)(2,1)} async-done(((bf16[512,1536]{1,0:T(8,128)(2,1)}), bf16[2048,1536]{1,0:T(8,128)(2,1)}) %all-gather.9.cloned.1.call-update) | async-done | bytes 6291472 | tf_op jit(solution)/shard_map/all_gather | solution.py:121
  188.3 8.5 convolution_add_fusion.1
  215.0 20.5 %all-gather.15.cloned.1.call-done = bf16[512,2048]{1,0:T(8,128)(2,1)} async-done(((bf16[512,512]{1,0:T(8,128)(2,1)}), bf16[512,2048]{1,0:T(8,128)(2,1)}) %all-gather.15.cloned.1.call-update) | async-done | bytes 2097168 | tf_op jit(solution)/shard_map/all_gather | solution.py:158
  235.5 105.9 %all-gather.11.cloned.1.call-done = bf16[2560,2048]{1,0:T(8,128)(2,1)} async-done(((bf16[2560,512]{1,0:T(8,128)(2,1)}), bf16[2560,2048]{1,0:T(8,128)(2,1)}) %all-gather.11.cloned.1.call-update) | async-done | bytes 10485776 | tf_op jit(solution)/shard_map/all_gather | solution.py:151
  341.4 9.5 convolution_bitcast_fusion.1
  356.2 3.4 multiply_reduce_fusion.1
  369.7 5.1 convolution_bitcast_fusion.2
  374.8 6.4 fusion.50
  381.2 7.3 all-gather.13.cloned.1.call-done
  388.5 12.9 %fusion.44 = (f32[2048]{0:T(1024)S(1)}, bf16[512,2048]{1,0:T(8,128)(2,1)S(1)}, f32[512,2048]{1,0:T(8,128)}) fusion(f32[2048]{0:T(1024)S(1)} %copy-done.42, f32[512,2560]{1,0:T(8,128)} %copy-done.28, bf16[512,2048]{1,0:T(8,128)(2,1)} %all-gather.13.cloned.1.call-done, bf16[1024,2048]{1,0:T(8,128)(2,1)} %collective-permute-done.1, ...), kind=kOutput, calls=%fused_computation.99 | convolution fusion | flops 4345296896 | bytes 20987904 | tf_op jit(solution)/shard_map/dot_general | solution.py:124
  401.5 8.6 fusion.30
  410.1 8.3 convolution_bitcast_fusion
  418.4 34.2 %pad_maximum_fusion = f32[2048,6144]{0,1:T(8,128)} fusion(f32[2048,2048]{0,1:T(8,128)} %convolution_bitcast_fusion, f32[2048,512]{0,1:T(8,128)S(1)} %copy-done, f32[2048,2048]{0,1:T(8,128)} %fusion.30, f32[2048,1536]{0,1:T(8,128)} %fusion.50), kind=kLoop, calls=%fused_computation | loop fusion | flops 37748736 | bytes 100663296 | tf_op jit(solution)/shard_map/concatenate | solution.py:233
  452.6 76.3 %all-gather.17.cloned.1.call-done = bf16[2048,3584]{1,0:T(8,128)(2,1)} async-done(((bf16[512,3584]{1,0:T(8,128)(2,1)}), bf16[2048,3584]{1,0:T(8,128)(2,1)}) %all-gather.17.cloned.1.call-update) | async-done | bytes 14680080 | tf_op jit(solution)/shard_map/all_gather | solution.py:213
  528.9 6.2 fusion.17
  535.2 7.0 fusion.20
  542.1 3.8 pad_maximum_fusion.1
  546.2 9.5 fusion.2
  555.7 5.0 convolution_add_fusion
  560.7 395.2 %reduce-scatter.8.cloned.1.call-done = f32[512,6144]{0,1:T(8,128)} async-done(((f32[2048,6144]{0,1:T(8,128)}), f32[512,6144]{0,1:T(8,128)}) %reduce-scatter.8.cloned.1.call-update) | async-done | bytes 12582928 | tf_op jit(solution)/shard_map/reduce_scatter | solution.py:232
  957.6 145.4 %reduce-scatter.6.cloned.1.call-done = f32[2,512,512]{2,1,0:T(8,128)} async-done(((f32[2,512,2048]{2,1,0:T(8,128)}), f32[2,512,512]{2,1,0:T(8,128)}) %reduce-scatter.6.cloned.1.call-update) | async-done | bytes 2097168 | tf_op jit(solution)/shard_map/reduce_scatter | solution.py:259
  1107.0 27.5 %all-reduce = (f32[512]{0:T(512)}, f32[512]{0:T(512)}, f32[512]{0:T(512)}, f32[512]{0:T(512)}, f32[1536]{0:T(1024)}, /*index=5*/f32[512]{0:T(512)S(1)}, f32[2048]{0:T(1024)}) all-reduce(f32[512]{0:T(512)S(1)} %get-tuple-element.120, f32[512]{0:T(512)S(1)} %get-tuple-element.122, ...), channel_id=1, replica_groups=mesh['dp'=2,'row'=4,'col'=4] {'dp','row'}, use_global_device_ids=true, to_apply=%region_14.15 | all-reduce | flops 6144 | bytes 49152 | tf_op jit(solution)/shard_map/psum | solution.py:270
  1134.4 12.4 all-reduce.1
  1146.8 36.8 %reduce-scatter.4.cloned.1.call-done = f32[512,512]{1,0:T(8,128)} async-done(((f32[512,2048]{1,0:T(8,128)}), f32[512,512]{1,0:T(8,128)}) %reduce-scatter.4.cloned.1.call-update) | async-done | bytes 1048592 | tf_op jit(solution)/shard_map/reduce_scatter | solution.py:155
  1186.5 50.0 %all-reduce.5.cloned.1.call-done = f32[512,6144]{0,1:T(8,128)} async-done(((f32[512,6144]{0,1:T(8,128)}), f32[512,6144]{0,1:T(8,128)}) %all-reduce.5.cloned.1.call-update) | async-done | bytes 12582928 | tf_op jit(solution)/shard_map/psum | solution.py:254
  1240.7 7.8 slice_bitcast_fusion
  1248.5 5.3 copy.89
  (158 shorter events, 61.6 us)
Async XLA Ops:
  7.2 18.6 %copy-start.6 = (f32[512,512]{1,0:T(8,128)S(1)}, f32[512,512]{1,0:T(8,128)}, u32[]{:S(2)}) copy-start(f32[512,512]{1,0:T(8,128)} %param.15) | copy-start | bytes 3145732
  7.2 20.1 %copy-start.27 = (bf16[512,512]{1,0:T(8,128)(2,1)S(1)}, bf16[512,512]{1,0:T(8,128)(2,1)}, u32[]{:S(2)}) copy-start(bf16[512,512]{1,0:T(8,128)(2,1)} %param.22) | copy-start | bytes 1572868
  7.2 80.3 %all-gather.7.cloned.1.call-start = ((), (), s32[]{:S(2)}) async-start(), calls=%async_computation.3 | async-start | bytes 2621440 | tf_op jit(solution)/shard_map/all_gather | solution.py:114
  25.0 163.3 %all-gather.9.cloned.1.call-start = ((), (), s32[]{:S(2)}) async-start(), calls=%async_computation.4 | async-start | bytes 7864320 | tf_op jit(solution)/shard_map/all_gather | solution.py:121
  25.7 209.8 %all-gather.15.cloned.1.call-start = ((), (), s32[]{:S(2)}) async-start(), calls=%async_computation.8 | async-start | bytes 2621440 | tf_op jit(solution)/shard_map/all_gather | solution.py:158
  27.3 314.2 %all-gather.11.cloned.1.call-start = ((), (), s32[]{:S(2)}) async-start(), calls=%async_computation.5 | async-start | bytes 13107200 | tf_op jit(solution)/shard_map/all_gather | solution.py:151
  30.7 357.8 %all-gather.13.cloned.1.call-start = ((), (), s32[]{:S(2)}) async-start(), calls=%async_computation.6 | async-start | bytes 2621440 | tf_op jit(solution)/shard_map/all_gather | solution.py:115
  31.3 497.6 %all-gather.17.cloned.1.call-start = ((), (), s32[]{:S(2)}) async-start(), calls=%async_computation.9 | async-start | bytes 18350080 | tf_op jit(solution)/shard_map/all_gather | solution.py:213
  35.1 920.9 %reduce-scatter.8.cloned.1.call-start = ((), (), s32[]{:S(2)}) async-start(), calls=%async_computation.11 | async-start | bytes 62914560 | tf_op jit(solution)/shard_map/reduce_scatter | solution.py:232
  35.1 46.1 %collective-permute-start = (bf16[512,2048]{1,0:T(8,128)(2,1)S(1)}, bf16[512,2048]{1,0:T(8,128)(2,1)}, u32[]{:S(2)}, u32[]{:S(2)}) collective-permute-start(bf16[512,2048]{1,0:T(8,128)(2,1)S(1)} %copy-done.3), channel_id=1, source_target_pairs={{0,4},{4,0},{8,12},{12,8},{1,5},{5,1},{9,13},{13,9},{2,6},{6,2},{1... | collective-permute-start | bytes 6291464 | tf_op jit(solution)/shard_map/ppermute | solution.py:20
  39.2 149.1 %copy-start.41 = (f32[1536]{0:T(1024)S(1)}, f32[1536]{0:T(1024)}, u32[]{:S(2)}) copy-start(f32[1536]{0:T(1024)} %param.21) | copy-start | bytes 18436
  86.4 302.1 %collective-permute-start.1 = (bf16[1024,2048]{1,0:T(8,128)(2,1)}, bf16[1024,2048]{1,0:T(8,128)(2,1)}, u32[]{:S(2)}, u32[]{:S(2)}) collective-permute-start(bf16[1024,2048]{1,0:T(8,128)(2,1)} %maximum_select_fusion.2), channel_id=1, source_target_pairs={{0,8},{4,12},{8,0},{12,4},{1,9},{5,13},{9,1},{13,5},{2,10},{6,14},... | collective-permute-start | bytes 12582920 | tf_op jit(solution)/shard_map/ppermute | solution.py:20
  374.8 13.7 %copy-start.42 = (f32[2048]{0:T(1024)S(1)}, f32[2048]{0:T(1024)}, u32[]{:S(2)}) copy-start(f32[2048]{0:T(1024)} %param.25) | copy-start | bytes 24580
  388.5 12.9 %copy-start.40 = (bf16[512,2048]{1,0:T(8,128)(2,1)S(1)}, bf16[512,2048]{1,0:T(8,128)(2,1)}, u32[]{:S(2)}) copy-start(bf16[512,2048]{1,0:T(8,128)(2,1)} %all-gather.13.cloned.1.call-done) | copy-start | bytes 6291460
  401.4 8.6 copy-start.43
  401.4 8.6 copy-start.13
  401.4 8.6 copy-start.45
  410.1 8.3 copy-start
  452.5 650.4 %reduce-scatter.6.cloned.1.call-start = ((), (), s32[]{:S(2)}) async-start(), calls=%async_computation.10 | async-start | bytes 10485760 | tf_op jit(solution)/shard_map/reduce_scatter | solution.py:259
  528.9 6.2 copy-start.44
  546.0 637.6 %reduce-scatter.4.cloned.1.call-start = ((), (), s32[]{:S(2)}) async-start(), calls=%async_computation.7 | async-start | bytes 5242880 | tf_op jit(solution)/shard_map/reduce_scatter | solution.py:155
  560.7 675.8 %all-reduce.5.cloned.1.call-start = ((), (), s32[]{:S(2)}) async-start(), calls=%async_computation.12 | async-start | bytes 25165824 | tf_op jit(solution)/shard_map/psum | solution.py:254
  956.0 148.7 %copy-start.1 = (f32[512,512]{1,0:T(8,128)S(1)}, f32[512,512]{1,0:T(8,128)}, u32[]{:S(2)}) copy-start(f32[512,512]{1,0:T(8,128)} %param.14) | copy-start | bytes 3145732
  956.0 148.7 %copy-start.30 = (f32[512]{0:T(512)S(1)}, f32[512]{0:T(512)}, u32[]{:S(2)}) copy-start(f32[512]{0:T(512)} %copy-done.29) | copy-start | bytes 6148
  956.0 148.7 %copy-start.32 = (f32[512]{0:T(512)S(1)}, f32[512]{0:T(512)}, u32[]{:S(2)}) copy-start(f32[512]{0:T(512)} %copy-done.31) | copy-start | bytes 6148
  956.0 148.7 %copy-start.34 = (f32[512]{0:T(512)S(1)}, f32[512]{0:T(512)}, u32[]{:S(2)}) copy-start(f32[512]{0:T(512)} %param.16) | copy-start | bytes 6148
  956.1 148.7 %copy-start.35 = (f32[512]{0:T(512)S(1)}, f32[512]{0:T(512)}, u32[]{:S(2)}) copy-start(f32[512]{0:T(512)} %param.18) | copy-start | bytes 6148
  956.1 150.9 %copy-start.33 = (f32[512]{0:T(512)S(1)}, f32[512]{0:T(512)}, u32[]{:S(2)}) copy-start(f32[512]{0:T(512)} %get-tuple-element.155) | copy-start | bytes 6148
  956.1 227.5 %copy-start.36 = (f32[512]{0:T(512)S(1)}, f32[512]{0:T(512)}, u32[]{:S(2)}) copy-start(f32[512]{0:T(512)} %param.27) | copy-start | bytes 6148
  956.1 227.5 %copy-start.37 = (f32[512]{0:T(512)S(1)}, f32[512]{0:T(512)}, u32[]{:S(2)}) copy-start(f32[512]{0:T(512)} %param.23) | copy-start | bytes 6148
  957.6 226.0 %copy-start.7 = (f32[512,512]{1,0:T(8,128)S(1)}, f32[512,512]{1,0:T(8,128)}, u32[]{:S(2)}) copy-start(f32[512,512]{1,0:T(8,128)} %param.15) | copy-start | bytes 3145732
  1134.4 121.6 %copy-start.38 = (f32[512]{0:T(512)}, f32[512]{0:T(512)S(1)}, u32[]{:S(2)}) copy-start(f32[512]{0:T(512)S(1)} %get-tuple-element.204) | copy-start | bytes 6148
  (27 other events, 90.3 us)
Sparse Core Ops, SparseCore 0:
  25.1 43.8 all-gather.6
  70.8 117.3 all-gather.8
  189.8 45.6 all-gather.14
  237.8 103.5 all-gather.10
  342.8 45.6 all-gather.12
  390.2 138.6 all-gather.16
  532.0 423.9 reduce-scatter.7
  958.3 144.6 reduce-scatter.5
  1105.9 77.6 reduce-scatter.3
  1185.9 50.5 all-reduce.4
